TPU v7x, 32 devices: a whole 2x2x4 slice. The times are simulated.
32 devices in a mesh: groups: 2 (over x), blk: 16 (over z, y, core).
Axes of the slice: x: 2, y: 2, z: 4, core: 2. Of those that a mesh axis runs over, the one named last changes fastest.
Arguments:
- embeddings: bfloat16 [12288, 512], P(('groups', 'blk')), parts along dimension 0, may hold values from -24 to 24
- cluster_ids: int32 [12288], P(('groups', 'blk')), parts along dimension 0, may hold values from 0 to 63, as said below
- cluster_sizes: int32 [128], P('groups'), parts along dimension 0, may hold values from 12 to 960, as said below
Outputs:
- log_density: float32 [12288], P(('groups', 'blk')), parts along dimension 0
- centrality: float32 [12288], P(('groups', 'blk')), parts along dimension 0
There are 2 independent parts, one for each index of `groups`. A program takes and returns all parts, laid end to end along the dimension named above; each array names one. Nothing has to cross between parts.
Inputs may be any that keep to these rules, and one draw needn't show every extreme that they name: cluster_sizes[c] is the number of rows whose cluster id is c; the sizes sum to 6144 and the largest is exactly 960. `cluster_ids`: rows are dealt to the devices of blk: with n the number of devices of blk and E_c the sum of cluster_sizes[c'] mod n over the clusters c' < c, device s holds cluster_sizes[c] // n rows of cluster c, plus one more exactly when (s - E_c) mod n < cluster_sizes[c] mod n. Within a device the rows stand in no particular order.
All inputs are finite; a program needn't handle non-finite values.
Results may differ from a plain program's by a relative error of at most 0.00065.
The roundings to bfloat16 on the way count: a program that leaves them out, or rounds other values in their place, can miss the bound.
Values may be sent and summed in bfloat16 or wider, within the bound.
No kernel may reach another device: no remote copies, remote signals or barrier semaphores. Data moves between devices by JAX's collectives and lax.ppermute only.
A program may use at most 64 MiB of HBM per device.

v0:
```python
import jax
import jax.numpy as jnp
from jax import lax
from jax.sharding import PartitionSpec as P

SOFTMAX_TEMP = 0.1
EPSILON = 1e-06


def shifted(array, axis, by):
    peers = lax.axis_size(axis)
    pairs = [(i, i + by) for i in range(peers) if 0 <= i + by < peers]
    return lax.ppermute(array, axis, pairs)


def unit_rows(embeddings):
    values = embeddings.astype(jnp.float32)
    scale = lax.rsqrt(jnp.mean(values * values, axis=1, keepdims=True) + EPSILON)
    return (values * (scale * values.shape[1] ** (-0.5))).astype(jnp.bfloat16)


def block_terms(remaining_rows, left_labels, right_rows, right_labels):
    similarity_scores = jnp.einsum(
        "rd,kd->rk", remaining_rows, right_rows, preferred_element_type=jnp.float32
    )
    same_cluster = left_labels[:, None] == right_labels[None, :]
    return jnp.sum(jnp.where(same_cluster, jnp.exp(similarity_scores / SOFTMAX_TEMP), 0.0), axis=1)


def lookup(table, one_hot):
    return jnp.sum(jnp.where(one_hot, table[None, :], 0), axis=1)


def sorted_density(unit, cluster_sizes, member):
    devices = lax.axis_size("blk")
    own_index = lax.axis_index("blk")
    rows_dev = unit.shape[0]
    clusters = cluster_sizes.shape[0]
    total_rows = rows_dev * devices
    fewest = total_rows // 512
    largest = total_rows * 5 // 32
    capacity = min(rows_dev, rows_dev // devices + rows_dev // fewest + 2)
    reach = (largest + rows_dev - 2) // rows_dev
    ends = jnp.cumsum(cluster_sizes)
    starts = ends - cluster_sizes
    base = cluster_sizes // devices
    extra = cluster_sizes % devices
    first = (jnp.cumsum(extra) - extra) % devices
    source_rows = jnp.arange(devices, dtype=jnp.int32)
    holds = base[None, :] + (
        (source_rows[:, None] - first[None, :]) % devices < extra[None, :]
    ).astype(jnp.int32)
    member_count = jnp.cumsum(member.astype(jnp.int32), axis=0)
    rank = jnp.sum(jnp.where(member, member_count - 1, 0), axis=1)
    held_row = jnp.dot(
        member.astype(jnp.float32), holds.T.astype(jnp.float32), precision=lax.Precision.HIGHEST
    ).astype(jnp.int32)
    before_me = (source_rows[None, :] < own_index) & (held_row > rank[:, None])
    within = jnp.sum(jnp.minimum(held_row, rank[:, None]), axis=1) + jnp.sum(
        before_me.astype(jnp.int32), axis=1
    )
    position = lookup(starts, member) + within
    target = position // rows_dev
    earlier = (target[None, :] == target[:, None]) & (position[None, :] < position[:, None])
    slot = jnp.sum(earlier.astype(jnp.int32), axis=1)
    address = target * capacity + slot
    sender = (
        jnp.zeros((devices * capacity,), jnp.int32)
        .at[address]
        .set(jnp.arange(rows_dev, dtype=jnp.int32))
    )
    filled = jnp.zeros((devices * capacity,), jnp.bool_).at[address].set(True)
    packed = jnp.where(filled[:, None], unit[sender], jnp.zeros((), jnp.bfloat16))
    arrived = lax.all_to_all(packed, "blk", split_axis=0, concat_axis=0, tiled=True)
    local = jnp.arange(rows_dev, dtype=jnp.int32)
    places = own_index * rows_dev + local
    home_label = jnp.sum((places[:, None] >= ends[None, :]).astype(jnp.int32), axis=1)
    home_cluster_member = home_label[:, None] == jnp.arange(clusters, dtype=jnp.int32)[None, :]
    offset_in = places - lookup(starts, home_cluster_member)
    base_row = lookup(base, home_cluster_member)
    extra_row = lookup(extra, home_cluster_member)
    first_row = lookup(first, home_cluster_member)
    full_rounds = devices * base_row
    surplus = offset_in - full_rounds
    wrapped = first_row + extra_row - devices
    late_source = jnp.where(
        wrapped > 0,
        jnp.where(surplus < wrapped, surplus, first_row + surplus - wrapped),
        first_row + surplus,
    )
    anchor = jnp.where(offset_in < full_rounds, offset_in % devices, late_source)
    anchor_hot = anchor[:, None] == source_rows[None, :]
    anchor_count = jnp.cumsum(anchor_hot.astype(jnp.int32), axis=0)
    order_in = jnp.sum(jnp.where(anchor_hot, anchor_count - 1, 0), axis=1)
    block = arrived[anchor * capacity + order_in]

    def labels_at(spots):
        inside = (spots >= 0) & (spots < total_rows)
        found = jnp.sum((spots[:, None] >= ends[None, :]).astype(jnp.int32), axis=1)
        return jnp.where(inside, found, -1)

    density = block_terms(block, home_label, block, home_label)

    def advance(offset, carried_rows):
        upper, lower, running = carried_rows
        upper = shifted(upper, "blk", 1)
        lower = shifted(lower, "blk", -1)
        running = running + block_terms(
            block, home_label, upper, labels_at(places - offset * rows_dev)
        )
        running = running + block_terms(
            block, home_label, lower, labels_at(places + offset * rows_dev)
        )
        return (upper, lower, running)

    carried_out = lax.fori_loop(1, reach + 1, advance, (block, block, density))
    density = carried_out[2]
    returned = (
        jnp.zeros((devices * capacity,), jnp.float32).at[anchor * capacity + order_in].set(density)
    )
    answered = lax.all_to_all(returned, "blk", split_axis=0, concat_axis=0, tiled=True)
    return answered[address]


def on_device(embeddings, cluster_ids, cluster_sizes):
    unit = unit_rows(embeddings)
    clusters = cluster_sizes.shape[0]
    member = cluster_ids[:, None] == jnp.arange(clusters, dtype=jnp.int32)[None, :]
    partial_sum = jnp.einsum(
        "rc,rd->cd", member.astype(jnp.bfloat16), unit, preferred_element_type=jnp.float32
    )
    centroid = lax.psum(partial_sum, "blk")
    density = sorted_density(unit, cluster_sizes, member)
    sizes_row = lookup(cluster_sizes, member).astype(jnp.float32)
    log_density = jnp.log(density / sizes_row)
    projected = jnp.dot(unit.astype(jnp.float32), centroid.T, precision=lax.Precision.HIGHEST)
    centrality = jnp.sum(jnp.where(member, projected, 0.0), axis=1) / sizes_row
    return (log_density, centrality)


def solution(mesh):
    in_specs = (P(("groups", "blk"), None), P(("groups", "blk")), P("groups"))
    out_specs = (P(("groups", "blk")), P(("groups", "blk")))
    return jax.shard_map(
        on_device, mesh=mesh, in_specs=in_specs, out_specs=out_specs, check_vma=False
    )
```

profile of v0, /device:TPU:0, one launch (start us, length us, event | category | flops | bytes accessed | tf_op | source)
XLA Modules:
  0.0 141.4 jit_solution(12733876175211087510)
XLA Ops:
  7.2 1.2 fusion.14
  8.4 0.1 fusion.15
  8.6 0.6 copy-done.2
  9.7 0.1 reduce.1
  10.0 0.6 copy-done.1
  10.6 0.9 reduce-window.41
  11.5 0.2 slice_reduce_fusion
  11.7 0.2 select_reduce_fusion
  11.9 0.3 convert_reduce_fusion.4
  12.3 0.3 convert_reduce_fusion.2
  12.6 2.9 %scatter_custom_fusion.1 = s32[928]{0:T(1024)S(1)} fusion(s32[384]{0:T(512)S(1)} %fusion.58, s32[384]{0:T(512)S(1)} %iota.57, s32[]{:T(128)} %copy.40), kind=kCustom, calls=%fused_computation.120 | custom fusion | bytes 3716 | tf_op jit(solution)/shard_map/scatter | solution.py:70
  15.5 4.0 %gather_fusion = bf16[928,512]{1,0:T(8,128)(2,1)S(1)} fusion(bf16[384,512]{1,0:T(8,128)(2,1)S(1)} %fusion.15, s32[1024]{0:T(1024)S(1)} %pad_clamp_fusion.2), kind=kCustom, calls=%fused_computation | custom fusion | bytes 1904256 | tf_op jit(solution)/shard_map/gather | solution.py:73
  19.6 0.2 gather.12
  19.8 2.0 %scatter_custom_fusion = pred[928]{0:T(1024)(128)(4,1)S(1)} fusion(s32[384]{0:T(512)S(1)} %fusion.58, pred[384]{0:T(512)(128)(4,1)S(1)} %broadcast.470, pred[]{:T(512)} %constant.152.clone.1), kind=kCustom, calls=%fused_computation.132 | custom fusion | bytes 929 | tf_op jit(solution)/shard_map/scatter | solution.py:72
  21.9 1.2 broadcast_select_fusion
  23.1 7.4 %all-to-all-start = ((bf16[16,58,512]{2,1,0:T(8,128)(2,1)}), bf16[16,58,512]{2,1,0:T(8,128)(2,1)S(1)}, u32[]{:S(2)}, u32[]{:S(2)}) async-start(bf16[16,58,512]{2,1,0:T(8,128)(2,1)} %broadcast_select_fusion), calls=%async_computation | async-start | bytes 2097152 | tf_op jit(solution)/shard_map/all_to_all | solution.py:74
  30.6 0.8 fusion.18
  31.5 0.9 reduce-window.39
  32.4 0.2 slice_reduce_fusion.1
  32.8 21.2 %all-to-all-done = bf16[16,58,512]{2,1,0:T(8,128)(2,1)S(1)} async-done(((bf16[16,58,512]{2,1,0:T(8,128)(2,1)}), bf16[16,58,512]{2,1,0:T(8,128)(2,1)S(1)}, u32[]{:S(2)}, u32[]{:S(2)}) %all-to-all-start) | async-done | bytes 950304 | tf_op jit(solution)/shard_map/all_to_all | solution.py:74
  53.9 0.3 all_to_all.15
  54.2 2.1 %gather_fusion.1 = bf16[384,512]{1,0:T(8,128)(2,1)S(1)} fusion(bf16[928,512]{1,0:T(8,128)(2,1)S(1)} %all_to_all.15, s32[1024]{0:T(1024)S(1)} %pad_clamp_fusion.1), kind=kCustom, calls=%fused_computation.1 | custom fusion | bytes 787968 | tf_op jit(solution)/shard_map/gather | solution.py:95
  56.3 0.4 fusion.12
  56.8 34.5 %while.18 = (s32[]{:T(128)}, bf16[384,512]{1,0:T(8,128)(2,1)S(1)}, bf16[384,512]{1,0:T(8,128)(2,1)S(1)}, f32[384]{0:T(512)S(1)}, s32[384]{0:T(512)S(1)}, /*index...) while((s32[]{:T(128)}, bf16[384,512]{1,0:T(8,128)(2,1)S(1)}, ...), condition=%wide.region_26.27_spmd.clone, body=%wide.region_21.26_spmd.clone.sunk | while | flops 303321984 | bytes 6322649 | solution.py:116
  56.8 2.7 %collective-permute-start = (bf16[384,512]{1,0:T(8,128)(2,1)S(1)}, bf16[384,512]{1,0:T(8,128)(2,1)S(1)}, u32[]{:S(2)}, u32[]{:S(2)}) collective-permute-start(bf16[384,512]{1,0:T(8,128)(2,1)S(1)} %get-tuple-element.275), channel_id=1, source_target_pairs={{0,1},{1,2},{2,3},{3,4},{4,5},{5,6},{6,7},{7,8},{8,9},{9,10},{10,1... | collective-permute-start | bytes 1179656 | tf_op jit(solution)/shard_map/while/body/eval_jaxpr/ppermute | solution.py:13
  59.5 1.3 collective-permute-start.1
  60.9 2.8 %collective-permute-done.1 = bf16[384,512]{1,0:T(8,128)(2,1)S(1)} collective-permute-done((bf16[384,512]{1,0:T(8,128)(2,1)S(1)}, bf16[384,512]{1,0:T(8,128)(2,1)S(1)}, u32[]{:S(2)}, u32[]{:S(2)}) %collective-permute-start.1) | collective-permute-done | bytes 393248 | tf_op jit(solution)/shard_map/while/body/eval_jaxpr/ppermute | solution.py:13
  63.7 0.4 fusion.89
  64.1 0.4 fusion.90
  64.6 7.9 %collective-permute-start = (bf16[384,512]{1,0:T(8,128)(2,1)S(1)}, bf16[384,512]{1,0:T(8,128)(2,1)S(1)}, u32[]{:S(2)}, u32[]{:S(2)}) collective-permute-start(bf16[384,512]{1,0:T(8,128)(2,1)S(1)} %get-tuple-element.275), channel_id=1, source_target_pairs={{0,1},{1,2},{2,3},{3,4},{4,5},{5,6},{6,7},{7,8},{8,9},{9,10},{10,1... | collective-permute-start | bytes 1179656 | tf_op jit(solution)/shard_map/while/body/eval_jaxpr/ppermute | solution.py:13
  72.5 1.3 collective-permute-start.1
  74.0 2.2 %collective-permute-done.1 = bf16[384,512]{1,0:T(8,128)(2,1)S(1)} collective-permute-done((bf16[384,512]{1,0:T(8,128)(2,1)S(1)}, bf16[384,512]{1,0:T(8,128)(2,1)S(1)}, u32[]{:S(2)}, u32[]{:S(2)}) %collective-permute-start.1) | collective-permute-done | bytes 393248 | tf_op jit(solution)/shard_map/while/body/eval_jaxpr/ppermute | solution.py:13
  76.2 0.4 fusion.89
  76.6 0.4 fusion.90
  77.1 9.6 %collective-permute-start = (bf16[384,512]{1,0:T(8,128)(2,1)S(1)}, bf16[384,512]{1,0:T(8,128)(2,1)S(1)}, u32[]{:S(2)}, u32[]{:S(2)}) collective-permute-start(bf16[384,512]{1,0:T(8,128)(2,1)S(1)} %get-tuple-element.275), channel_id=1, source_target_pairs={{0,1},{1,2},{2,3},{3,4},{4,5},{5,6},{6,7},{7,8},{8,9},{9,10},{10,1... | collective-permute-start | bytes 1179656 | tf_op jit(solution)/shard_map/while/body/eval_jaxpr/ppermute | solution.py:13
  86.7 1.3 collective-permute-start.1
  88.2 2.2 %collective-permute-done.1 = bf16[384,512]{1,0:T(8,128)(2,1)S(1)} collective-permute-done((bf16[384,512]{1,0:T(8,128)(2,1)S(1)}, bf16[384,512]{1,0:T(8,128)(2,1)S(1)}, u32[]{:S(2)}, u32[]{:S(2)}) %collective-permute-start.1) | collective-permute-done | bytes 393248 | tf_op jit(solution)/shard_map/while/body/eval_jaxpr/ppermute | solution.py:13
  90.3 0.4 fusion.89
  90.8 0.4 fusion.90
  91.3 2.9 %scatter_custom_fusion.2 = f32[928]{0:T(1024)S(1)} fusion(s32[384]{0:T(512)S(1)} %fusion.57, f32[384]{0:T(512)S(1)} %get-tuple-element.141, f32[]{:T(128)} %constant.139.clone.1), kind=kCustom, calls=%fused_computation.128 | custom fusion | bytes 3716 | tf_op jit(solution)/shard_map/scatter | solution.py:119
  94.2 0.7 all_to_all.16
  94.9 14.2 %all-to-all-start.1 = ((f32[16,58,1]{1,2,0:T(1,128)}), f32[16,58,1]{1,2,0:T(1,128)S(1)}, u32[]{:S(2)}, u32[]{:S(2)}) async-start(f32[16,58,1]{1,2,0:T(1,128)} %bitcast.9), calls=%async_computation.1 | async-start | bytes 16384 | tf_op jit(solution)/shard_map/all_to_all | solution.py:121
  109.0 20.4 %all-reduce.2.cloned.1.call-done = f32[64,512]{1,0:T(8,128)} async-done(((f32[64,512]{1,0:T(8,128)}), f32[64,512]{1,0:T(8,128)}) %all-reduce.2.cloned.1.call-update) | async-done | bytes 131088 | tf_op jit(solution)/shard_map/psum | solution.py:132
  129.4 1.4 fusion.13
  130.8 0.5 broadcast.549
  131.3 0.7 reduce.13
  132.1 1.9 %gather_fusion.2 = f32[384]{0:T(512)S(1)} fusion(f32[928]{0:T(1024)S(1)} %all_to_all.18, s32[1024]{0:T(1024)S(1)} %pad_clamp_fusion), kind=kCustom, calls=%fused_computation.2 | custom fusion | bytes 4608 | tf_op jit(solution)/shard_map/gather | solution.py:122
  134.0 0.6 convert_divide_fusion
  (62 shorter events, 1.8 us)
Async XLA Ops:
  7.2 1.2 copy-start
  8.6 0.7 copy-start.2
  9.9 0.7 copy-start.1
  23.1 30.8 %all-to-all-start = ((bf16[16,58,512]{2,1,0:T(8,128)(2,1)}), bf16[16,58,512]{2,1,0:T(8,128)(2,1)S(1)}, u32[]{:S(2)}, u32[]{:S(2)}) async-start(bf16[16,58,512]{2,1,0:T(8,128)(2,1)} %broadcast_select_fusion), calls=%async_computation | async-start | bytes 2097152 | tf_op jit(solution)/shard_map/all_to_all | solution.py:74
  30.5 98.9 %all-reduce.2.cloned.1.call-start = ((), (), s32[]{:S(2)}) async-start(), calls=%async_computation.2 | async-start | bytes 262144 | tf_op jit(solution)/shard_map/psum | solution.py:132
  56.8 7.3 %collective-permute-start = (bf16[384,512]{1,0:T(8,128)(2,1)S(1)}, bf16[384,512]{1,0:T(8,128)(2,1)S(1)}, u32[]{:S(2)}, u32[]{:S(2)}) collective-permute-start(bf16[384,512]{1,0:T(8,128)(2,1)S(1)} %get-tuple-element.275), channel_id=1, source_target_pairs={{0,1},{1,2},{2,3},{3,4},{4,5},{5,6},{6,7},{7,8},{8,9},{9,10},{10,1... | collective-permute-start | bytes 1179656 | tf_op jit(solution)/shard_map/while/body/eval_jaxpr/ppermute | solution.py:13
  59.5 4.2 %collective-permute-start.1 = (bf16[384,512]{1,0:T(8,128)(2,1)S(1)}, bf16[384,512]{1,0:T(8,128)(2,1)S(1)}, u32[]{:S(2)}, u32[]{:S(2)}) collective-permute-start(bf16[384,512]{1,0:T(8,128)(2,1)S(1)} %get-tuple-element.276), channel_id=1, source_target_pairs={{1,0},{2,1},{3,2},{4,3},{5,4},{6,5},{7,6},{8,7},{9,8},{10,9},{11,1... | collective-permute-start | bytes 1179656 | tf_op jit(solution)/shard_map/while/body/eval_jaxpr/ppermute | solution.py:13
  64.6 12.0 %collective-permute-start = (bf16[384,512]{1,0:T(8,128)(2,1)S(1)}, bf16[384,512]{1,0:T(8,128)(2,1)S(1)}, u32[]{:S(2)}, u32[]{:S(2)}) collective-permute-start(bf16[384,512]{1,0:T(8,128)(2,1)S(1)} %get-tuple-element.275), channel_id=1, source_target_pairs={{0,1},{1,2},{2,3},{3,4},{4,5},{5,6},{6,7},{7,8},{8,9},{9,10},{10,1... | collective-permute-start | bytes 1179656 | tf_op jit(solution)/shard_map/while/body/eval_jaxpr/ppermute | solution.py:13
  72.5 3.6 %collective-permute-start.1 = (bf16[384,512]{1,0:T(8,128)(2,1)S(1)}, bf16[384,512]{1,0:T(8,128)(2,1)S(1)}, u32[]{:S(2)}, u32[]{:S(2)}) collective-permute-start(bf16[384,512]{1,0:T(8,128)(2,1)S(1)} %get-tuple-element.276), channel_id=1, source_target_pairs={{1,0},{2,1},{3,2},{4,3},{5,4},{6,5},{7,6},{8,7},{9,8},{10,9},{11,1... | collective-permute-start | bytes 1179656 | tf_op jit(solution)/shard_map/while/body/eval_jaxpr/ppermute | solution.py:13
  77.1 13.6 %collective-permute-start = (bf16[384,512]{1,0:T(8,128)(2,1)S(1)}, bf16[384,512]{1,0:T(8,128)(2,1)S(1)}, u32[]{:S(2)}, u32[]{:S(2)}) collective-permute-start(bf16[384,512]{1,0:T(8,128)(2,1)S(1)} %get-tuple-element.275), channel_id=1, source_target_pairs={{0,1},{1,2},{2,3},{3,4},{4,5},{5,6},{6,7},{7,8},{8,9},{9,10},{10,1... | collective-permute-start | bytes 1179656 | tf_op jit(solution)/shard_map/while/body/eval_jaxpr/ppermute | solution.py:13
  86.7 3.6 %collective-permute-start.1 = (bf16[384,512]{1,0:T(8,128)(2,1)S(1)}, bf16[384,512]{1,0:T(8,128)(2,1)S(1)}, u32[]{:S(2)}, u32[]{:S(2)}) collective-permute-start(bf16[384,512]{1,0:T(8,128)(2,1)S(1)} %get-tuple-element.276), channel_id=1, source_target_pairs={{1,0},{2,1},{3,2},{4,3},{5,4},{6,5},{7,6},{8,7},{9,8},{10,9},{11,1... | collective-permute-start | bytes 1179656 | tf_op jit(solution)/shard_map/while/body/eval_jaxpr/ppermute | solution.py:13
  94.9 36.0 %all-to-all-start.1 = ((f32[16,58,1]{1,2,0:T(1,128)}), f32[16,58,1]{1,2,0:T(1,128)S(1)}, u32[]{:S(2)}, u32[]{:S(2)}) async-start(f32[16,58,1]{1,2,0:T(1,128)} %bitcast.9), calls=%async_computation.1 | async-start | bytes 16384 | tf_op jit(solution)/shard_map/all_to_all | solution.py:121
Sparse Core Ops, SparseCore 0:
  34.8 94.5 all-reduce.1
where the time goes:
time: 143 us; the launch traced here: 141 us
  waiting for transfers between devices  48.7 us (34%)
  starting transfers between devices  45.7 us (32%)
  local copies, waits for them, and re-layouts  19.8 us (14%)
  between operations  14.3 us (10%)
  other arithmetic  7.29 us (5%)
  matrix products  5.4 us (4%)
    ppermute x6, starting transfers between devices, shifted(): return lax.ppermute(array, axis, pairs)  24.1 us
    all_to_all x1, waiting for transfers between devices, sorted_density(): lax.all_to_all(packed, 'blk', split_axis=0, concat_axis=0, tiled=True)  21.2 us
    psum x1, waiting for transfers between devices, on_device(): centroid = lax.psum(partial_sum, 'blk')  20.4 us
    all_to_all x1, starting transfers between devices, sorted_density(): lax.all_to_all(returned, 'blk', split_axis=0, concat_axis=0, tiled=True)  14.2 us
    all_to_all x1, starting transfers between devices, sorted_density(): lax.all_to_all(packed, 'blk', split_axis=0, concat_axis=0, tiled=True)  7.41 us
    ppermute x6, waiting for transfers between devices, shifted(): return lax.ppermute(array, axis, pairs)  7.15 us
    gather x2, local copies, waits for them, and re-layouts, sorted_density(): unit[sender]  4.29 us
    scatter x1, local copies, waits for them, and re-layouts, sorted_density(): sender = jnp.zeros((devices * capacity,), jnp.int32).at[address].set(jnp....  2.92 us
  transfers between devices with their start and end apart: 9, of which 5 were waited for; matrix products, arithmetic and copies ran while one was open for 8% of the time, Pallas kernels for 0%

commit v1 on v0

v1 whole, which is shorter than its diff:
```python
import functools

import jax
import jax.numpy as jnp
from jax import lax
from jax.experimental import pallas as pl
from jax.experimental.pallas import tpu as pltpu
from jax.sharding import PartitionSpec as P

SOFTMAX_TEMP = 0.1
EPSILON = 1e-06
LANES = 128
CORES = 2
F32 = jnp.float32
BF16 = jnp.bfloat16
FAR = 4096.0


def iota(shape, dim):
    return lax.broadcasted_iota(jnp.int32, shape, dim)


def pick(mask, values, axis):
    return jnp.sum(jnp.where(mask, values, 0.0), axis=axis, keepdims=True)


def one_hot(mask):
    return jnp.where(mask, 1.0, 0.0).astype(BF16)


def matmul(a, b):
    return jnp.dot(a, b, preferred_element_type=F32)


def bin_capacity(rows_dev, devices, clusters):
    total = rows_dev * devices
    largest, fewest = total * 5 // 32, total // 512
    bins = devices // CORES
    heaviest = -(-largest // devices)
    first = devices * (heaviest - 1) + 1
    bound = heaviest
    for k in range(bins + 1, clusters + 1):
        rest = total - first - fewest * (clusters - k)
        for weight in range(1, heaviest + 1):
            least = max(devices * (weight - 1) + 1, fewest)
            if (k - 1) * least > rest:
                break
            others = (rest - least + (devices - 1) * (k - 2)) // devices
            bound = max(bound, others // (bins - 1) + weight)
    return -(-bound // 8) * 8


def held(start, size, device, devices):
    last = jnp.floor((start + size - device + (devices - 1)) * (1.0 / devices))
    return last - jnp.floor((start - device + (devices - 1)) * (1.0 / devices))


def pack_kernel(devices, cap, emb, ids, sizes, send, place, bins_out, weights, picks):
    rows, width = emb.shape
    clusters = sizes.shape[1]
    bins = devices // CORES
    me = lax.axis_index("blk").astype(F32)
    values = emb[...].astype(F32)
    scale = lax.rsqrt(jnp.mean(values * values, axis=1, keepdims=True) + EPSILON)
    unit = (values * (scale * width ** (-0.5))).astype(BF16)

    size = sizes[...].astype(F32)
    down, across = iota((clusters, clusters), 0), iota((clusters, clusters), 1)
    size_col = pick(down == across, size, 1)
    start = pick(down < across, size_col, 0)
    weight = jnp.floor((size + (devices - 1)) * (1.0 / devices))
    weight_col = jnp.floor((size_col + (devices - 1)) * (1.0 / devices))
    key = weight * clusters - across[:1].astype(F32)
    key_col = weight_col * clusters - down[:, :1].astype(F32)
    rank = pick(key_col > key, 1.0, 0)
    ranked = rank == down.astype(F32)
    weights[...] = jnp.broadcast_to(pick(ranked, weight, 1), weights.shape) * bins

    bin_id = iota((bins, LANES), 0).astype(F32)
    load = weights[:bins, :] + bin_id
    picks[:bins, :] = bin_id
    for t in range(bins, clusters):
        least = jnp.min(load, axis=0, keepdims=True)
        picks[t : t + 1, :] = least
        load = jnp.where(load == least, load + weights[t : t + 1, :], load)
    chosen = picks[...]
    chosen = (chosen - jnp.floor(chosen * (1.0 / bins)) * bins)[:, :clusters]
    of_bin = pick(ranked, chosen, 0)
    bins_out[...] = of_bin
    of_bin_col = pick(down == across, of_bin, 1)
    hold = held(start, size, me, devices)
    offset = pick((of_bin == of_bin_col) & (across < down), hold, 1)
    base = of_bin_col * cap + offset

    member = ids[...] == iota((clusters, rows), 0)
    earlier = one_hot(iota((rows, rows), 0) < iota((rows, rows), 1))
    order = matmul(one_hot(member), earlier)
    target = pick(member, order + base, 0)
    place[...] = target
    slots = bins * cap
    put = one_hot(iota((slots, rows), 0).astype(F32) == target)
    send[...] = matmul(put, unit).astype(BF16)


def pair_sums(left, left_label, right, right_label, chunk):
    density, agreement = 0.0, 0.0
    for at in range(0, left.shape[0], chunk):
        cosine = lax.dot_general(
            left[at : at + chunk, :],
            right,
            (((1,), (1,)), ((), ())),
            preferred_element_type=F32,
        )
        same = left_label[at : at + chunk, :] == right_label
        terms = jnp.where(same, jnp.exp(cosine * (1.0 / SOFTMAX_TEMP)), 0.0)
        density = density + jnp.sum(terms, axis=0, keepdims=True)
        agreement = agreement + jnp.sum(jnp.where(same, cosine, 0.0), axis=0, keepdims=True)
    return density, agreement


def own_kernel(devices, cap, chunk, mine, sizes, bins_in, sums, label_row, label_col):
    clusters = sizes.shape[1]
    bins = devices // CORES
    slots = bins * cap
    me = lax.axis_index("blk")
    core = lax.rem(me, CORES)
    chip = ((me - core) // CORES).astype(F32)
    size = sizes[...].astype(F32)
    down, across = iota((clusters, clusters), 0), iota((clusters, clusters), 1)
    size_col = pick(down == across, size, 1)
    start = pick(down < across, size_col, 0)
    inside = bins_in[...] == chip
    inside_col = pick((down == across) & inside, 1.0, 1) > 0.0

    def row_labels(parity):
        start_col = pick(across < down, size, 1)
        source = (iota((clusters, bins), 1) * CORES + parity).astype(F32)
        hold = held(start_col, size_col, source, devices).astype(BF16)
        upto = one_hot((across <= down) & inside)
        ends = jnp.where(inside_col, matmul(upto, hold), FAR).astype(BF16)
        low = iota((bins, slots), 0) * cap
        spot = iota((bins, slots), 1)
        block = (spot >= low) & (spot < low + cap)
        slot = pick(block, (spot - low).astype(F32), 0)
        return pick(matmul(ends, one_hot(block)) <= slot, 1.0, 0)

    def col_labels(parity):
        source = (iota((bins, clusters), 0) * CORES + parity).astype(F32)
        hold = held(start, size, source, devices).astype(BF16)
        upto = one_hot((down <= across) & inside_col)
        ends = jnp.where(inside, matmul(hold, upto), FAR).astype(BF16)
        low = iota((slots, bins), 1) * cap
        spot = iota((slots, bins), 0)
        block = (spot >= low) & (spot < low + cap)
        slot = pick(block, (spot - low).astype(F32), 1)
        return pick(matmul(one_hot(block), ends) <= slot, 1.0, 1)

    label = row_labels(core)
    label_row[...] = label
    label_col[...] = jnp.broadcast_to(col_labels(CORES - 1 - core), label_col.shape)
    density, agreement = pair_sums(mine, col_labels(core), mine[...], label, chunk)
    sums[0:1, :] = density
    sums[1:2, :] = agreement


def mate_kernel(bins, cap, chunk, other, mine, sums, label_row, label_col, out):
    density, agreement = pair_sums(other, label_col[:, :1], mine[...], label_row[...], chunk)
    density = density + sums[0:1, :]
    agreement = agreement + sums[1:2, :]
    out[...] = jnp.zeros(out.shape, F32)
    for b in range(bins):
        out[b, 0:1, :cap] = density[:, b * cap : (b + 1) * cap]
        out[b, 1:2, :cap] = agreement[:, b * cap : (b + 1) * cap]


def finish_kernel(bins, cap, back, place, ids, sizes, log_density, centrality):
    rows = ids.shape[1]
    clusters = sizes.shape[1]
    size = sizes[...].astype(F32)
    size_col = pick(iota((clusters, clusters), 0) == iota((clusters, clusters), 1), size, 1)
    size_row = pick(ids[...] == iota((clusters, rows), 0), size_col, 0)
    target = place[...]
    low = (iota((bins, rows), 0) * cap).astype(F32)
    here = (target >= low) & (target < low + cap)
    slot = pick(here, target - low, 0)
    lane = one_hot(iota((LANES, rows), 0).astype(F32) == slot)

    def fetch(values):
        high = values.astype(BF16)
        left = values - high.astype(F32)
        mid = left.astype(BF16)
        low_part = (left - mid.astype(F32)).astype(BF16)
        found = (matmul(low_part, lane) + matmul(mid, lane)) + matmul(high, lane)
        return pick(here, found, 0)

    log_density[...] = jnp.log(fetch(back[:, 0, :]) / size_row)
    centrality[...] = fetch(back[:, 1, :]) / size_row


def call(kernel, out, operands, scratch=(), flops=0, name=None):
    return pl.pallas_call(
        kernel,
        out_shape=out,
        in_specs=[pl.BlockSpec(memory_space=pltpu.VMEM)] * len(operands),
        out_specs=jax.tree.map(lambda _: pl.BlockSpec(memory_space=pltpu.VMEM), out),
        scratch_shapes=scratch,
        cost_estimate=pl.CostEstimate(flops=flops, bytes_accessed=0, transcendentals=0),
        name=name,
    )(*operands)


def chunk_of(slots):
    for parts in range(1, slots + 1):
        if slots % (8 * parts) == 0 and slots // parts <= 256:
            return slots // parts
    return slots


def on_device(embeddings, cluster_ids, cluster_sizes):
    devices = lax.axis_size("blk")
    rows, width = embeddings.shape
    clusters = cluster_sizes.shape[0]
    bins = devices // CORES
    cap = bin_capacity(rows, devices, clusters)
    slots = bins * cap
    chunk = chunk_of(slots)
    lanes = [[CORES * b + core for b in range(bins)] for core in range(CORES)]
    ids = cluster_ids.reshape(1, rows)
    sizes = cluster_sizes.reshape(1, clusters)

    def shape(*dims, dtype=F32):
        return jax.ShapeDtypeStruct(dims, dtype)

    send, place, of_bin = call(
        functools.partial(pack_kernel, devices, cap),
        (shape(slots, width, dtype=BF16), shape(1, rows), shape(1, clusters)),
        (embeddings, ids, sizes),
        scratch=[pltpu.VMEM((clusters, LANES), F32), pltpu.VMEM((clusters, LANES), F32)],
        name="pack",
    )
    mine = lax.all_to_all(
        send.reshape(bins, cap, width), "blk", 0, 0, tiled=True, axis_index_groups=lanes
    ).reshape(slots, width)
    other = lax.ppermute(mine, "blk", [(i, i ^ 1) for i in range(devices)])
    sums, label_row, label_col = call(
        functools.partial(own_kernel, devices, cap, chunk),
        (shape(2, slots), shape(1, slots), shape(slots, LANES)),
        (mine, sizes, of_bin),
        flops=2 * slots * slots * width,
        name="own",
    )
    out = call(
        functools.partial(mate_kernel, bins, cap, chunk),
        shape(bins, 2, LANES),
        (other, mine, sums, label_row, label_col),
        flops=2 * slots * slots * width,
        name="mate",
    )
    back = lax.all_to_all(out, "blk", 0, 0, tiled=True, axis_index_groups=lanes)
    log_density, centrality = call(
        functools.partial(finish_kernel, bins, cap),
        (shape(1, rows), shape(1, rows)),
        (back, place, ids, sizes),
        name="finish",
    )
    return log_density.reshape(rows), centrality.reshape(rows)


def solution(mesh):
    in_specs = (P(("groups", "blk"), None), P(("groups", "blk")), P("groups"))
    out_specs = (P(("groups", "blk")), P(("groups", "blk")))
    return jax.shard_map(
        on_device, mesh=mesh, in_specs=in_specs, out_specs=out_specs, check_vma=False
    )
```

time: 143 us -> 51.1 us (0.36)
  waiting for transfers between devices: 48.7 us -> 0.01 us
  starting transfers between devices: 45.7 us -> 0.01 us
  blocking collectives: 0 us -> 34.2 us
  local copies, waits for them, and re-layouts: 19.8 us -> 4.16 us
  between operations: 14.3 us -> 0.64 us
  Pallas kernels: 0 us -> 10.4 us
  other arithmetic: 7.29 us -> 1.19 us
  matrix products: 5.4 us -> 0 us
    all_to_all x0 -> x2, blocking collectives: none -> 34.2 us  [the longest x1 23.8 us: on_device(): lax.all_to_all(send.reshape(bins, cap, width), 'blk', 0, 0, tiled=True, a...]
    ppermute x6 -> x1, starting transfers between devices: 24.1 us -> 0.01 us  [on_device(): other = lax.ppermute(mine, 'blk', [(i, i ^ 1) for i in range(devices)])]
    all_to_all x2 -> x0, starting transfers between devices: 21.6 us -> none  [the longest x1 14.2 us: sorted_density(): lax.all_to_all(returned, 'blk', split_axis=0, concat_axis=0, tiled=True)]
    all_to_all x2 -> x0, waiting for transfers between devices: 21.2 us -> none  [the longest x1 21.2 us: sorted_density(): lax.all_to_all(packed, 'blk', split_axis=0, concat_axis=0, tiled=True)]
    psum x1 -> x0, waiting for transfers between devices: 20.4 us -> none  [on_device(): centroid = lax.psum(partial_sum, 'blk')]
    pallas_call x0 -> x4, Pallas kernels: none -> 10.4 us  [call(): pl.pallas_call(kernel, out_shape=out, in_specs=[pl.BlockSpec(memory_space...]
    gather x4 -> x0, local copies, waits for them, and re-layouts: 8.25 us -> none  [the longest x2 4.29 us: sorted_density(): unit[sender]]
    scatter x3 -> x0, local copies, waits for them, and re-layouts: 7.81 us -> none  [the longest x1 2.92 us: sorted_density(): sender = jnp.zeros((devices * capacity,), jnp.int32).at[address].set(jnp....]
  transfers between devices with their start and end apart: 9 -> 1, of which waited for: 5 -> 0; matrix products, arithmetic and copies ran while one was open for 8% -> 0% of each run, Pallas kernels for 0% -> 6%
where the time goes in v1:
time: 51.1 us; the launch traced here: 50.7 us
  blocking collectives  34.2 us (67%)
  Pallas kernels  10.4 us (20%)
  local copies, waits for them, and re-layouts  4.16 us (8%)
  other arithmetic  1.19 us (2%)
  between operations  0.64 us (1%)
    all_to_all x1, blocking collectives, on_device(): lax.all_to_all(send.reshape(bins, cap, width), 'blk', 0, 0, tiled=True, a...  23.8 us
    pallas_call x4, Pallas kernels, call(): pl.pallas_call(kernel, out_shape=out, in_specs=[pl.BlockSpec(memory_space...  10.4 us
    all_to_all x1, blocking collectives, on_device(): back = lax.all_to_all(out, 'blk', 0, 0, tiled=True, axis_index_groups=lanes)  10.4 us
    unnamed x8, local copies, waits for them, and re-layouts  2.91 us
    reshape x1, local copies, waits for them, and re-layouts, on_device(): ids = cluster_ids.reshape(1, rows)  1.25 us
    pallas_call x2, other arithmetic, call(): pl.pallas_call(kernel, out_shape=out, in_specs=[pl.BlockSpec(memory_space...  1.19 us
  transfers between devices with their start and end apart: 1, of which 0 were waited for; matrix products, arithmetic and copies ran while one was open for 0% of the time, Pallas kernels for 6%

profile of v1, /device:TPU:0, one launch (start us, length us, event | category | flops | bytes accessed | tf_op | source)
XLA Modules:
  0.0 50.7 jit_solution(9995935597362531740)
XLA Ops:
  0.6 1.2 %reshape.22.ids = s32[1,384]{1,0:T(1,128)} reshape(s32[384]{0:T(512)} %param.4) | data formatting | bytes 3072 | tf_op jit(solution)/shard_map/reshape | solution.py:228
  1.9 3.1 %pack.1 = (bf16[576,512]{1,0:T(8,128)(2,1)}, f32[1,384]{1,0:T(1,128)}, f32[1,64]{1,0:T(1,128)}) custom-call(bf16[384,512]{1,0:T(8,128)(2,1)} %emb.1, s32[1,384]{1,0:T(1,128)} %reshape.22.ids, s32[1,64]{1,0:T(1,128)} %bitcast.7), custom_call_target="tpu_custom_call" | custom-call | tf_op jit(solution)/shard_map/pack/pallas_call | solution.py:201
  5.0 23.8 %all_to_all.10 = bf16[8,72,512]{2,1,0:T(8,128)(2,1)S(1)} all-to-all(bf16[8,72,512]{2,1,0:T(8,128)(2,1)} %bitcast.6), channel_id=1, replica_groups={{0,2,4,6,8,10,12,14},{1,3,5,7,9,11,13,15},{16,18,20,22,24,26,28,30},{17..., dimensions={0} | all-to-all | bytes 1179648 | tf_op jit(solution)/shard_map/all_to_all | solution.py:241
  28.8 0.0 copy-start
  28.8 0.0 collective-permute-start
  28.8 0.8 %copy-done = bf16[8,72,512]{2,1,0:T(8,128)(2,1)} copy-done((bf16[8,72,512]{2,1,0:T(8,128)(2,1)}, bf16[8,72,512]{2,1,0:T(8,128)(2,1)S(1)}, u32[]{:S(2)}) %copy-start) | copy-done | bytes 589848
  29.6 3.0 %own.1 = (f32[2,576]{1,0:T(2,128)}, f32[1,576]{1,0:T(1,128)}, f32[576,128]{1,0:T(8,128)}) custom-call(bf16[576,512]{1,0:T(8,128)(2,1)} %bitcast.4, s32[1,64]{1,0:T(1,128)} %bitcast.8, f32[1,64]{1,0:T(1,128)} %get-tuple-element.11.bins_in), custom_call_target="tpu_custom_call" | custom-call | flops 339738624 | tf_op jit(solution)/shard_map/own/pallas_call | solution.py:201
  32.6 0.0 collective-permute-done.other
  32.6 0.0 copy-start.1
  32.6 0.8 %copy-done.1 = bf16[576,512]{1,0:T(8,128)(2,1)} copy-done((bf16[576,512]{1,0:T(8,128)(2,1)}, bf16[576,512]{1,0:T(8,128)(2,1)S(1)}, u32[]{:S(2)}) %copy-start.1) | copy-done | bytes 589848
  33.4 2.9 %mate.1 = f32[8,2,128]{2,1,0:T(2,128)} custom-call(bf16[576,512]{1,0:T(8,128)(2,1)} %copy-done.1, bf16[576,512]{1,0:T(8,128)(2,1)} %bitcast.5, f32[2,576]{1,0:T(2,128)} %get-tuple-element.12.sums, f32[1,576]{1,0:T(1,128)} %get-tuple-element.13.label_row, f32[576,128]{1,0:T(8,128)} %get-tuple-element.14.label_col), custom_call_target="tpu_custom_call" | custom-call | flops 339738624 | tf_op jit(solution)/shard_map/mate/pallas_call | solution.py:201
  36.2 10.4 %all_to_all.11.back = f32[8,2,128]{2,1,0:T(2,128)} all-to-all(f32[8,2,128]{2,1,0:T(2,128)} %mate.1), channel_id=1, replica_groups={{0,2,4,6,8,10,12,14},{1,3,5,7,9,11,13,15},{16,18,20,22,24,26,28,30},{17..., dimensions={0} | all-to-all | bytes 16384 | tf_op jit(solution)/shard_map/all_to_all | solution.py:259
  46.6 1.5 %finish.1 = (f32[1,384]{1,0:T(1,128)}, f32[1,384]{1,0:T(1,128)}) custom-call(f32[8,2,128]{2,1,0:T(2,128)} %all_to_all.11.back, f32[1,384]{1,0:T(1,128)} %get-tuple-element.15.place, s32[1,384]{1,0:T(1,128)} %reshape.22.ids, s32[1,64]{1,0:T(1,128)} %bitcast.9), custom_call_target="tpu_custom_call" | custom-call | tf_op jit(solution)/shard_map/finish/pallas_call | solution.py:201
  48.2 0.0 copy-start.3
  48.2 0.6 %copy-done.3 = f32[1,384]{1,0:T(1,128)S(1)} copy-done((f32[1,384]{1,0:T(1,128)S(1)}, f32[1,384]{1,0:T(1,128)}, u32[]{:S(2)}) %copy-start.3) | copy-done | bytes 1560
  48.8 0.6 %reduce = f32[384]{0:T(512)} reduce(f32[1,384]{1,0:T(1,128)S(1)} %copy-done.3, f32[]{:T(128)} %constant), dimensions={0}, to_apply=%get-tuple-element.16.reduce_sub_computation | reduce | bytes 3076 | tf_op jit(solution)/shard_map/finish/pallas_call | solution.py:201
  49.4 0.0 copy-start.2
  49.4 0.7 %copy-done.2 = f32[1,384]{1,0:T(1,128)S(1)} copy-done((f32[1,384]{1,0:T(1,128)S(1)}, f32[1,384]{1,0:T(1,128)}, u32[]{:S(2)}) %copy-start.2) | copy-done | bytes 1560
  50.1 0.6 %reduce.1 = f32[384]{0:T(512)} reduce(f32[1,384]{1,0:T(1,128)S(1)} %copy-done.2, f32[]{:T(128)} %constant), dimensions={0}, to_apply=%get-tuple-element.17.reduce_sub_computation | reduce | bytes 3076 | tf_op jit(solution)/shard_map/finish/pallas_call | solution.py:201
Async XLA Ops:
  28.8 0.8 %copy-start = (bf16[8,72,512]{2,1,0:T(8,128)(2,1)}, bf16[8,72,512]{2,1,0:T(8,128)(2,1)S(1)}, u32[]{:S(2)}) copy-start(bf16[8,72,512]{2,1,0:T(8,128)(2,1)S(1)} %all_to_all.10) | copy-start | bytes 1769476
  28.8 3.8 %collective-permute-start = (bf16[576,512]{1,0:T(8,128)(2,1)S(1)}, bf16[576,512]{1,0:T(8,128)(2,1)S(1)}, u32[]{:S(2)}, u32[]{:S(2)}) collective-permute-start(bf16[576,512]{1,0:T(8,128)(2,1)S(1)} %bitcast.3), channel_id=1, source_target_pairs={{0,1},{1,0},{2,3},{3,2},{4,5},{5,4},{6,7},{7,6},{8,9},{9,8},{10,11... | collective-permute-start | bytes 1769480 | tf_op jit(solution)/shard_map/ppermute | solution.py:244
  32.6 0.8 %copy-start.1 = (bf16[576,512]{1,0:T(8,128)(2,1)}, bf16[576,512]{1,0:T(8,128)(2,1)S(1)}, u32[]{:S(2)}) copy-start(bf16[576,512]{1,0:T(8,128)(2,1)S(1)} %collective-permute-done.other) | copy-start | bytes 1769476
  48.2 0.6 %copy-start.3 = (f32[1,384]{1,0:T(1,128)S(1)}, f32[1,384]{1,0:T(1,128)}, u32[]{:S(2)}) copy-start(f32[1,384]{1,0:T(1,128)} %get-tuple-element.16) | copy-start | bytes 4612
  49.4 0.7 %copy-start.2 = (f32[1,384]{1,0:T(1,128)S(1)}, f32[1,384]{1,0:T(1,128)}, u32[]{:S(2)}) copy-start(f32[1,384]{1,0:T(1,128)} %get-tuple-element.17) | copy-start | bytes 4612

commit v2 on v1

--- a/solution.py
+++ b/solution.py
@@ -14,6 +14,7 @@
 F32 = jnp.float32
 BF16 = jnp.bfloat16
 FAR = 4096.0
+VMEM_LIMIT = 24 * 1024 * 1024
 
 
 def iota(shape, dim):
@@ -57,14 +58,14 @@
 
 def pack_kernel(devices, cap, emb, ids, sizes, send, place, bins_out, weights, picks):
     rows, width = emb.shape
-    clusters = sizes.shape[1]
+    clusters = sizes.shape[0]
     bins = devices // CORES
     me = lax.axis_index("blk").astype(F32)
     values = emb[...].astype(F32)
     scale = lax.rsqrt(jnp.mean(values * values, axis=1, keepdims=True) + EPSILON)
     unit = (values * (scale * width ** (-0.5))).astype(BF16)
 
-    size = sizes[...].astype(F32)
+    size = sizes[...].reshape(1, clusters).astype(F32)
     down, across = iota((clusters, clusters), 0), iota((clusters, clusters), 1)
     size_col = pick(down == across, size, 1)
     start = pick(down < across, size_col, 0)
@@ -92,7 +93,7 @@
     offset = pick((of_bin == of_bin_col) & (across < down), hold, 1)
     base = of_bin_col * cap + offset
 
-    member = ids[...] == iota((clusters, rows), 0)
+    member = ids[...].reshape(1, rows) == iota((clusters, rows), 0)
     earlier = one_hot(iota((rows, rows), 0) < iota((rows, rows), 1))
     order = matmul(one_hot(member), earlier)
     target = pick(member, order + base, 0)
@@ -119,13 +120,13 @@
 
 
 def own_kernel(devices, cap, chunk, mine, sizes, bins_in, sums, label_row, label_col):
-    clusters = sizes.shape[1]
+    clusters = sizes.shape[0]
     bins = devices // CORES
     slots = bins * cap
     me = lax.axis_index("blk")
     core = lax.rem(me, CORES)
     chip = ((me - core) // CORES).astype(F32)
-    size = sizes[...].astype(F32)
+    size = sizes[...].reshape(1, clusters).astype(F32)
     down, across = iota((clusters, clusters), 0), iota((clusters, clusters), 1)
     size_col = pick(down == across, size, 1)
     start = pick(down < across, size_col, 0)
@@ -174,11 +175,11 @@
 
 
 def finish_kernel(bins, cap, back, place, ids, sizes, log_density, centrality):
-    rows = ids.shape[1]
-    clusters = sizes.shape[1]
-    size = sizes[...].astype(F32)
+    rows = ids.shape[0]
+    clusters = sizes.shape[0]
+    size = sizes[...].reshape(1, clusters).astype(F32)
     size_col = pick(iota((clusters, clusters), 0) == iota((clusters, clusters), 1), size, 1)
-    size_row = pick(ids[...] == iota((clusters, rows), 0), size_col, 0)
+    size_row = pick(ids[...].reshape(1, rows) == iota((clusters, rows), 0), size_col, 0)
     target = place[...]
     low = (iota((bins, rows), 0) * cap).astype(F32)
     here = (target >= low) & (target < low + cap)
@@ -193,8 +194,8 @@
         found = (matmul(low_part, lane) + matmul(mid, lane)) + matmul(high, lane)
         return pick(here, found, 0)
 
-    log_density[...] = jnp.log(fetch(back[:, 0, :]) / size_row)
-    centrality[...] = fetch(back[:, 1, :]) / size_row
+    log_density[...] = jnp.log(fetch(back[:, 0, :]) / size_row).reshape(rows)
+    centrality[...] = (fetch(back[:, 1, :]) / size_row).reshape(rows)
 
 
 def call(kernel, out, operands, scratch=(), flops=0, name=None):
@@ -205,6 +206,7 @@
         out_specs=jax.tree.map(lambda _: pl.BlockSpec(memory_space=pltpu.VMEM), out),
         scratch_shapes=scratch,
         cost_estimate=pl.CostEstimate(flops=flops, bytes_accessed=0, transcendentals=0),
+        compiler_params=pltpu.CompilerParams(vmem_limit_bytes=VMEM_LIMIT),
         name=name,
     )(*operands)
 
@@ -225,8 +227,7 @@
     slots = bins * cap
     chunk = chunk_of(slots)
     lanes = [[CORES * b + core for b in range(bins)] for core in range(CORES)]
-    ids = cluster_ids.reshape(1, rows)
-    sizes = cluster_sizes.reshape(1, clusters)
+    ids, sizes = cluster_ids, cluster_sizes
 
     def shape(*dims, dtype=F32):
         return jax.ShapeDtypeStruct(dims, dtype)
@@ -259,11 +260,11 @@
     back = lax.all_to_all(out, "blk", 0, 0, tiled=True, axis_index_groups=lanes)
     log_density, centrality = call(
         functools.partial(finish_kernel, bins, cap),
-        (shape(1, rows), shape(1, rows)),
+        (shape(rows), shape(rows)),
         (back, place, ids, sizes),
         name="finish",
     )
-    return log_density.reshape(rows), centrality.reshape(rows)
+    return log_density, centrality
 
 
 def solution(mesh):

time: 51.1 us -> 41.2 us (0.81)
  Pallas kernels: 10.4 us -> 4.29 us
  local copies, waits for them, and re-layouts: 4.16 us -> 2.32 us
  blocking collectives: 34.2 us -> 33 us
  other arithmetic: 1.19 us -> 0 us
  waiting for transfers between devices: 0.01 us -> 0.71 us
    pallas_call x4, Pallas kernels: 10.4 us -> 4.29 us  [call(): pl.pallas_call(kernel, out_shape=out, in_specs=[pl.BlockSpec(memory_space...]
    reshape x1 -> x0, local copies, waits for them, and re-layouts: 1.25 us -> none  [on_device(): ids = cluster_ids.reshape(1, rows)]
    pallas_call x2 -> x0, other arithmetic: 1.19 us -> none  [call(): pl.pallas_call(kernel, out_shape=out, in_specs=[pl.BlockSpec(memory_space...]
    all_to_all x1, blocking collectives: 10.4 us -> 9.32 us  [on_device(): back = lax.all_to_all(out, 'blk', 0, 0, tiled=True, axis_index_groups=lanes)]
    ppermute x1, waiting for transfers between devices: 0.01 us -> 0.71 us  [on_device(): other = lax.ppermute(mine, 'blk', [(i, i ^ 1) for i in range(devices)])]
    unnamed x8 -> x6, local copies, waits for them, and re-layouts: 2.91 us -> 2.32 us
  transfers between devices with their start and end apart: 1 -> 1, of which waited for: 0 -> 1; matrix products, arithmetic and copies ran while one was open for 0% -> 0% of each run, Pallas kernels for 6% -> 3%
where the time goes in v2:
time: 41.2 us; the launch traced here: 40.9 us
  blocking collectives  33 us (80%)
  Pallas kernels  4.29 us (10%)
  local copies, waits for them, and re-layouts  2.32 us (6%)
  waiting for transfers between devices  0.71 us (2%)
  between operations  0.66 us (2%)
    all_to_all x1, blocking collectives, on_device(): lax.all_to_all(send.reshape(bins, cap, width), 'blk', 0, 0, tiled=True, a...  23.6 us
    all_to_all x1, blocking collectives, on_device(): back = lax.all_to_all(out, 'blk', 0, 0, tiled=True, axis_index_groups=lanes)  9.32 us
    pallas_call x4, Pallas kernels, call(): pl.pallas_call(kernel, out_shape=out, in_specs=[pl.BlockSpec(memory_space...  4.29 us
    unnamed x6, local copies, waits for them, and re-layouts  2.32 us
  transfers between devices with their start and end apart: 1, of which 1 were waited for; matrix products, arithmetic and copies ran while one was open for 0% of the time, Pallas kernels for 3%

profile of v2, /device:TPU:0, one launch (start us, length us, event | category | flops | bytes accessed | tf_op | source)
XLA Modules:
  0.0 40.9 jit_solution(6882369294663472757)
XLA Ops:
  0.6 0.0 copy-start
  0.6 1.0 %copy-done = bf16[384,512]{1,0:T(8,128)(2,1)S(1)} copy-done((bf16[384,512]{1,0:T(8,128)(2,1)S(1)}, bf16[384,512]{1,0:T(8,128)(2,1)}, u32[]{:S(2)}) %copy-start) | copy-done | bytes 393240
  1.6 0.0 copy-start.1
  1.6 0.7 %copy-done.1 = s32[384]{0:T(512)S(1)} copy-done((s32[384]{0:T(512)S(1)}, s32[384]{0:T(512)}, u32[]{:S(2)}) %copy-start.1) | copy-done | bytes 1560
  2.3 0.0 copy-start.2
  2.3 0.7 %copy-done.2 = s32[64]{0:T(128)S(1)} copy-done((s32[64]{0:T(128)S(1)}, s32[64]{0:T(128)}, u32[]{:S(2)}) %copy-start.2) | copy-done | bytes 280
  3.0 1.2 %pack.1 = (bf16[576,512]{1,0:T(8,128)(2,1)S(1)}, f32[1,384]{1,0:T(1,128)S(1)}, f32[1,64]{1,0:T(1,128)S(1)}) custom-call(bf16[384,512]{1,0:T(8,128)(2,1)S(1)} %copy-done, s32[384]{0:T(512)S(1)} %copy-done.1, s32[64]{0:T(128)S(1)} %copy-done.2), custom_call_target="tpu_custom_call" | custom-call | tf_op jit(solution)/shard_map/pack/pallas_call | solution.py:202
  4.2 23.6 %all_to_all.10 = bf16[8,72,512]{2,1,0:T(8,128)(2,1)S(1)} all-to-all(bf16[8,72,512]{2,1,0:T(8,128)(2,1)S(1)} %bitcast.5), channel_id=1, replica_groups={{0,2,4,6,8,10,12,14},{1,3,5,7,9,11,13,15},{16,18,20,22,24,26,28,30},{17..., dimensions={0} | all-to-all | bytes 1179648 | tf_op jit(solution)/shard_map/all_to_all | solution.py:242
  27.9 0.0 collective-permute-start
  27.9 1.3 %own.1 = (f32[2,576]{1,0:T(2,128)S(1)}, f32[1,576]{1,0:T(1,128)S(1)}, f32[576,128]{1,0:T(8,128)S(1)}) custom-call(bf16[576,512]{1,0:T(8,128)(2,1)S(1)} %bitcast.3, s32[64]{0:T(128)S(1)} %copy-done.2, f32[1,64]{1,0:T(1,128)S(1)} %get-tuple-element.9.bins_in), custom_call_target="tpu_custom_call" | custom-call | flops 339738624 | tf_op jit(solution)/shard_map/own/pallas_call | solution.py:202
  29.1 0.7 %collective-permute-done.other = bf16[576,512]{1,0:T(8,128)(2,1)S(1)} collective-permute-done((bf16[576,512]{1,0:T(8,128)(2,1)S(1)}, bf16[576,512]{1,0:T(8,128)(2,1)S(1)}, u32[]{:S(2)}, u32[]{:S(2)}) %collective-permute-start) | collective-permute-done | bytes 589856 | tf_op jit(solution)/shard_map/ppermute | solution.py:245
  29.9 0.9 %mate.1 = f32[8,2,128]{2,1,0:T(2,128)S(1)} custom-call(bf16[576,512]{1,0:T(8,128)(2,1)S(1)} %collective-permute-done.other, bf16[576,512]{1,0:T(8,128)(2,1)S(1)} %bitcast.4, f32[2,576]{1,0:T(2,128)S(1)} %get-tuple-element.10.sums, f32[1,576]{1,0:T(1,128)S(1)} %get-tuple-element.11.label_row, f32[576,128]{1,0:T(8,128)S(1)} %get-tuple-element.12.label_col), custom_call_target="tpu_custom_call" | custom-call | flops 339738624 | tf_op jit(solution)/shard_map/mate/pallas_call | solution.py:202
  30.8 9.3 %all_to_all.11.back = f32[8,2,128]{2,1,0:T(2,128)S(1)} all-to-all(f32[8,2,128]{2,1,0:T(2,128)S(1)} %mate.1), channel_id=1, replica_groups={{0,2,4,6,8,10,12,14},{1,3,5,7,9,11,13,15},{16,18,20,22,24,26,28,30},{17..., dimensions={0} | all-to-all | bytes 16384 | tf_op jit(solution)/shard_map/all_to_all | solution.py:260
  40.1 0.8 %finish.1 = (f32[384]{0:T(512)}, f32[384]{0:T(512)}) custom-call(f32[8,2,128]{2,1,0:T(2,128)S(1)} %all_to_all.11.back, f32[1,384]{1,0:T(1,128)S(1)} %get-tuple-element.13.place, s32[384]{0:T(512)S(1)} %copy-done.1, s32[64]{0:T(128)S(1)} %copy-done.2), custom_call_target="tpu_custom_call" | custom-call | tf_op jit(solution)/shard_map/finish/pallas_call | solution.py:202
Async XLA Ops:
  0.6 1.0 %copy-start = (bf16[384,512]{1,0:T(8,128)(2,1)S(1)}, bf16[384,512]{1,0:T(8,128)(2,1)}, u32[]{:S(2)}) copy-start(bf16[384,512]{1,0:T(8,128)(2,1)} %emb.1) | copy-start | bytes 1179652
  1.6 0.7 %copy-start.1 = (s32[384]{0:T(512)S(1)}, s32[384]{0:T(512)}, u32[]{:S(2)}) copy-start(s32[384]{0:T(512)} %ids.3) | copy-start | bytes 4612
  2.3 0.7 %copy-start.2 = (s32[64]{0:T(128)S(1)}, s32[64]{0:T(128)}, u32[]{:S(2)}) copy-start(s32[64]{0:T(128)} %sizes.5) | copy-start | bytes 772
  27.9 2.0 %collective-permute-start = (bf16[576,512]{1,0:T(8,128)(2,1)S(1)}, bf16[576,512]{1,0:T(8,128)(2,1)S(1)}, u32[]{:S(2)}, u32[]{:S(2)}) collective-permute-start(bf16[576,512]{1,0:T(8,128)(2,1)S(1)} %bitcast.2), channel_id=1, source_target_pairs={{0,1},{1,0},{2,3},{3,2},{4,5},{5,4},{6,7},{7,6},{8,9},{9,8},{10,11... | collective-permute-start | bytes 1769480 | tf_op jit(solution)/shard_map/ppermute | solution.py:245
